TPU v7x, 32 devices: a whole 2x2x4 slice. The times are simulated.
32 devices in a mesh: groups: 1, role: 2 (over core), dev: 16 (over z, y, x).
Axes of the slice: x: 2, y: 2, z: 4, core: 2. Of those that a mesh axis runs over, the one named last changes fastest.
Arguments:
- prompt_hidden: bfloat16 [4096, 4096], P(('groups', 'dev')), may hold values from -6 to 6
- norm_gain: float32 [4096], replicated, may hold values from 0.25 to 1.75
- kv_weight: bfloat16 [4096, 4, 2, 128], P(None, 'role'), may hold values from -0.09375 to 0.09375
- prompt_excess: int32 [4], P('groups'), may hold values from 1 to 1536, 2048 in all
- prompt_owner: int32 [4], P('groups'), may hold values from 0 to 15, as said below
- response_counts: int32 [4], P('groups'), may hold values from 1 to 5, as said below
- queries: bfloat16 [256, 16, 128], P(('groups', 'dev'), 'role'), may hold values from -256 to 256
- new_kv: bfloat16 [256, 4, 2, 128], P(('groups', 'dev'), 'role'), may hold values from -6 to 6
- response_cache: bfloat16 [256, 256, 4, 2, 128], P(('groups', 'dev'), None, 'role'), may hold values from -6 to 6
- positions: int32 [256], P(('groups', 'dev')), may hold values from 0 to 256
- out_weight: bfloat16 [16, 128, 4096], P('role', None, 'dev'), may hold values from -0.125 to 0.125
Outputs:
- attended: bfloat16 [256, 16, 128], P(('groups', 'dev'), 'role')
- block_out: bfloat16 [256, 4096], P(('groups', 'role'), 'dev')
Inputs may be any that keep to these rules, and one draw needn't show every extreme that they name: `prompt_owner`: no device along dev owns more than two prompts, and some device owns exactly two. `response_counts`: some prompt has exactly 5 responses.
All inputs are finite; a program needn't handle non-finite values.
Results may differ from a plain program's by a relative error of at most 0.0065.
Values may be sent and summed in bfloat16 or wider, within the bound.
No kernel may reach another device: no remote copies, remote signals or barrier semaphores. Data moves between devices by JAX's collectives and lax.ppermute only.
A program may use at most 192 MiB of HBM per device.

v0:
```python
import jax
import jax.numpy as jnp
from jax import lax
from jax.sharding import PartitionSpec as P

RESP = 5
PROMPT_MIN = 512
rope_base = 500000.0


def merged_2(part, axis, combine):
    gathered = jax.tree.map(lambda a: lax.all_gather(a, axis), part)

    def take(source):
        return jax.tree.map(lambda a: lax.dynamic_index_in_dim(a, source, 0, False), gathered)

    return lax.fori_loop(
        1, lax.axis_size(axis), lambda source, state: combine(state, take(source)), take(0)
    )


def rotate(vectors, offsets):
    half = vectors.shape[-1] // 2
    freq = rope_base ** (-jnp.arange(half, dtype=jnp.float32) * 2.0 / vectors.shape[-1])
    angles = offsets.astype(jnp.float32)[:, None] * freq[None, :]
    cosine = jnp.cos(angles)[:, None, :]
    sine = jnp.sin(angles)[:, None, :]
    first = vectors[..., :half]
    second = vectors[..., half:]
    return jnp.concatenate(
        [first * cosine - second * sine, second * cosine + first * sine], axis=-1
    )


def prompt_layout(prompt_excess, token_index):
    lengths = PROMPT_MIN + prompt_excess
    ends = jnp.cumsum(lengths)
    starts = ends - lengths
    prompt_id = jnp.sum((token_index[:, None] >= ends[None, :]).astype(jnp.int32), axis=1)
    member = prompt_id[:, None] == jnp.arange(lengths.shape[0], dtype=jnp.int32)[None, :]
    offsets = token_index - jnp.sum(jnp.where(member, starts[None, :], 0), axis=1)
    return (member, offsets, starts, lengths)


def first_slots(owner, counts):
    order = jnp.arange(owner.shape[0], dtype=jnp.int32)
    earlier = (owner[:, None] == owner[None, :]) & (order[None, :] < order[:, None])
    return jnp.sum(jnp.where(earlier, counts[None, :], 0), axis=1)


def slot_prompts(owner, counts, slot_device, slot_index):
    order = jnp.arange(owner.shape[0], dtype=jnp.int32)
    first = first_slots(owner, counts)
    match = (
        (owner[None, :] == slot_device[:, None])
        & (first[None, :] <= slot_index[:, None])
        & (slot_index[:, None] < first[None, :] + counts[None, :])
    )
    present = jnp.any(match, axis=1)
    chosen = jnp.sum(jnp.where(match, order[None, :], 0), axis=1)
    return (chosen, present)


def softmax_state(scores, valid):
    scores = jnp.where(valid[:, None, None, :], scores, -1e30)
    peak = jnp.max(scores, axis=-1)
    weights = jnp.where(valid[:, None, None, :], jnp.exp(scores - peak[..., None]), 0.0)
    return (peak, jnp.sum(weights, axis=-1), weights.astype(jnp.bfloat16))


def state_each(query, keys, values, valid, scale):
    scores = jnp.einsum("sngd,slnd->sngl", query, keys, preferred_element_type=jnp.float32) * scale
    peak, total, rounded = softmax_state(scores, valid)
    mixed = jnp.einsum("sngl,slnd->sngd", rounded, values, preferred_element_type=jnp.float32)
    return (peak, total, mixed)


def state_shared(query, keys, values, valid, scale):
    scores = jnp.einsum("sngd,lnd->sngl", query, keys, preferred_element_type=jnp.float32) * scale
    peak, total, rounded = softmax_state(scores, valid)
    mixed = jnp.einsum("sngl,lnd->sngd", rounded, values, preferred_element_type=jnp.float32)
    return (peak, total, mixed)


def combine(first, second):
    peak = jnp.maximum(first[0], second[0])
    left_scale = jnp.exp(first[0] - peak)
    right_scale = jnp.exp(second[0] - peak)
    total = first[1] * left_scale + second[1] * right_scale
    mixed = first[2] * left_scale[..., None] + second[2] * right_scale[..., None]
    return (peak, total, mixed)


def on_device(
    prompt_hidden,
    norm_gain,
    kv_weight,
    prompt_excess,
    prompt_owner,
    response_counts,
    queries,
    new_kv,
    response_cache,
    positions,
    out_weight,
):
    device = lax.axis_index("dev")
    rows = prompt_hidden.shape[0]
    width = prompt_hidden.shape[1]
    local_heads = kv_weight.shape[1]
    head_size = kv_weight.shape[3]
    slots = queries.shape[0]
    query_heads = queries.shape[1]
    group = query_heads // local_heads
    prompt_count = prompt_excess.shape[0]
    scale = head_size ** (-0.5)
    token_index = device * rows + jnp.arange(rows, dtype=jnp.int32)
    member, offsets, starts, lengths = prompt_layout(prompt_excess, token_index)
    hidden = prompt_hidden.astype(jnp.float32)
    normed = (
        hidden * lax.rsqrt(jnp.mean(hidden * hidden, axis=-1, keepdims=True) + 1e-05) * norm_gain
    ).astype(jnp.bfloat16)
    projected = jnp.dot(
        normed,
        kv_weight.reshape(width, local_heads * 2 * head_size),
        preferred_element_type=jnp.float32,
    )
    projected = projected.reshape(rows, local_heads, 2, head_size)
    prompt_keys = rotate(projected[:, :, 0], offsets).astype(jnp.bfloat16)
    prompt_values = projected[:, :, 1].astype(jnp.bfloat16)
    grouped = queries.reshape(slots, local_heads, group, head_size)
    slot_index = jnp.arange(slots, dtype=jnp.int32)
    chosen, present = slot_prompts(
        prompt_owner, response_counts, jnp.zeros((slots,), jnp.int32) + device, slot_index
    )
    cache_valid = jnp.arange(response_cache.shape[1], dtype=jnp.int32)[None, :] < positions[:, None]
    cache_state = state_each(
        grouped, response_cache[:, :, :, 0], response_cache[:, :, :, 1], cache_valid, scale
    )
    self_valid = jnp.ones((slots, 1), dtype=bool)
    self_state = state_each(
        grouped, new_kv[:, None, :, 0], new_kv[:, None, :, 1], self_valid, scale
    )
    first = first_slots(prompt_owner, response_counts)
    rank = jnp.clip(slot_index - first[chosen], 0, RESP - 1)
    entry = chosen * RESP + rank
    select = (
        (entry[None, :] == jnp.arange(prompt_count * RESP, dtype=jnp.int32)[:, None])
        & present[None, :]
    ).astype(jnp.float32)
    table = jnp.dot(
        select,
        queries.reshape(slots, query_heads * head_size).astype(jnp.float32),
        precision=lax.Precision.HIGHEST,
    )
    table = lax.psum(table, "dev").astype(jnp.bfloat16)
    table = table.reshape(prompt_count, RESP, local_heads, group, head_size)
    held = jnp.any(member, axis=0)
    first_prompt = jnp.sum((starts + lengths <= token_index[0]).astype(jnp.int32))
    reach = min(rows // PROMPT_MIN + 2, prompt_count)
    layout = (
        jnp.full((prompt_count, RESP, local_heads, group), -1e30, jnp.float32),
        jnp.zeros((prompt_count, RESP, local_heads, group), jnp.float32),
        jnp.zeros((prompt_count, RESP, local_heads, group, head_size), jnp.float32),
    )
    for step in range(reach):
        pick = jnp.minimum(first_prompt + step, prompt_count - 1)
        live = (first_prompt + step < prompt_count) & held[pick]
        reply_queries = lax.dynamic_index_in_dim(table, pick, 0, keepdims=False)
        reply_live = jnp.arange(RESP, dtype=jnp.int32) < response_counts[pick]
        row_member = (token_index >= starts[pick]) & (token_index < starts[pick] + lengths[pick])
        valid = live & reply_live[:, None] & row_member[None, :]
        fresh = state_shared(reply_queries, prompt_keys, prompt_values, valid, scale)
        earlier = tuple(
            (lax.dynamic_index_in_dim(part_now, pick, 0, keepdims=False) for part_now in layout)
        )
        merged = combine(earlier, fresh)
        layout = tuple(
            (
                lax.dynamic_update_index_in_dim(part_now, part_new, pick, 0)
                for part_now, part_new in zip(layout, merged)
            )
        )
    joined_peak, joined_total, joined_mixed = merged_2(layout, "dev", combine)
    flat_peak = joined_peak.reshape(prompt_count * RESP, local_heads, group)
    flat_total = joined_total.reshape(prompt_count * RESP, local_heads, group)
    flat_mixed = joined_mixed.reshape(prompt_count * RESP, local_heads, group, head_size)
    own_peak = jnp.take(flat_peak, entry, axis=0)
    own_total = jnp.take(flat_total, entry, axis=0)
    own_mixed = jnp.take(flat_mixed, entry, axis=0)
    prompt_state = (
        jnp.where(present[:, None, None], own_peak, -1e30),
        jnp.where(present[:, None, None], own_total, 0.0),
        jnp.where(present[:, None, None, None], own_mixed, 0.0),
    )
    final = combine(combine(prompt_state, cache_state), self_state)
    attended = (
        (final[2] / final[1][..., None]).reshape(slots, query_heads, head_size).astype(jnp.bfloat16)
    )
    flat = attended.reshape(slots, query_heads * head_size)
    weight_flat = out_weight.reshape(query_heads * head_size, out_weight.shape[2])
    head_terms = jnp.dot(
        lax.all_gather(flat, "dev", axis=0, tiled=True),
        weight_flat,
        preferred_element_type=jnp.float32,
    )
    block_out = lax.psum_scatter(head_terms, "role", scatter_dimension=0, tiled=True).astype(
        jnp.bfloat16
    )
    return (attended, block_out)


def solution(mesh):
    return jax.shard_map(
        on_device,
        mesh=mesh,
        in_specs=(
            P(("groups", "dev"), None),
            P(),
            P(None, "role", None, None),
            P("groups"),
            P("groups"),
            P("groups"),
            P(("groups", "dev"), "role", None),
            P(("groups", "dev"), "role", None, None),
            P(("groups", "dev"), None, "role", None, None),
            P(("groups", "dev")),
            P("role", None, "dev"),
        ),
        out_specs=(P(("groups", "dev"), "role", None), P(("groups", "role"), "dev")),
        check_vma=False,
    )
```

profile of v0, /device:TPU:0, one launch (start us, length us, event | category | flops | bytes accessed | tf_op | source)
XLA Modules:
  0.0 298.8 jit_solution(10407446676272909244)
XLA Ops:
  7.8 0.7 broadcast_add_fusion
  8.6 1.9 bitcast_subtract_fusion.3
  11.8 0.7 broadcast_compare_fusion
  12.5 0.9 select_reduce_fusion.2
  13.4 1.3 fusion.107
  14.8 0.6 fusion.110
  16.3 0.7 fusion.109
  17.0 0.6 fusion.108
  17.6 0.7 add.228
  18.4 0.7 gather_fusion
  19.0 0.9 fusion.46
  19.9 79.5 %psum.7 = bf16[20,1024]{1,0:T(8,128)(2,1)S(1)} all-reduce(f32[20,1024]{1,0:T(8,128)S(1)} %fusion.46), channel_id=1, replica_groups=mesh['groups'=1,'role'=2,'dev'=16] {'dev'}, use_global_device_ids=true, to_apply=%region_9.10 | all-reduce | flops 20480 | bytes 122880 | tf_op jit(solution)/shard_map/psum | solution.py:156
  99.5 7.2 %reshape.412 = bf16[4096,512]{1,0:T(8,128)(2,1)} reshape(bf16[4096,2,2,128]{3,2,1,0:T(2,128)(2,1)} %param.17) | data formatting | bytes 8388608 | tf_op jit(solution)/shard_map/reshape | solution.py:125
  106.7 6.6 %copy.138 = bf16[512,4096]{1,0:T(8,128)(2,1)} copy(bf16[512,4096]{0,1:T(8,128)(2,1)} %bitcast.222) | data formatting | bytes 8388608 | tf_op jit(solution)/shard_map/dot_general | solution.py:123
  113.8 3.6 %fusion.7 = f32[256,2,2,128]{0,3,2,1:T(8,128)S(1)} fusion(bf16[2,2,128,4096]{3,2,1,0:T(8,128)(2,1)} %bitcast.223, bf16[256,4096]{1,0:T(8,128)(2,1)S(1)} %copy-done.1, f32[4096]{0:T(1024)S(1)} %copy-done.7, f32[256]{0:T(256)S(1)} %add_rsqrt_fusion), kind=kOutput, calls=%fused_computation.18 | convolution fusion | flops 1077936128 | bytes 6833152 | tf_op jit(solution)/shard_map/dot_general | solution.py:123
  119.9 1.2 compare_and_fusion
  122.0 0.6 compare_and_fusion.3
  124.1 0.6 compare_and_fusion.1
  125.3 0.6 copy-done.2
  126.0 10.2 %fusion.106 = (bf16[16,256,2,1,128]{4,3,2,1,0:T(2,128)(2,1)}, bf16[16,256,2,1,128]{4,3,2,1,0:T(2,128)(2,1)}) fusion(bf16[16,256,2,2,128]{4,3,2,1,0:T(2,128)(2,1)} %param.23), kind=kLoop, calls=%fused_computation.189 | loop fusion | bytes 8388608 | tf_op jit(solution)/shard_map/slice | solution.py:138
  136.3 2.9 fusion.111
  140.1 37.8 %all_gather.32 = f32[16,4,5,2,4]{2,4,3,1,0:T(4,128)S(1)} all-gather(f32[1,4,5,2,4]{2,4,3,1,0:T(4,128)S(1)} %get-tuple-element.219), channel_id=1, replica_groups=mesh['groups'=1,'role'=2,'dev'=16] {'dev'}, dimensions={0}, use_global_device_ids=true | all-gather | bytes 10880 | tf_op jit(solution)/shard_map/all_gather | solution.py:12
  177.9 38.5 %all_gather.29 = f32[16,4,5,2,4]{2,4,3,1,0:T(4,128)S(1)} all-gather(f32[1,4,5,2,4]{2,4,3,1,0:T(4,128)S(1)} %get-tuple-element.220), channel_id=1, replica_groups=mesh['groups'=1,'role'=2,'dev'=16] {'dev'}, dimensions={0}, use_global_device_ids=true | all-gather | bytes 10880 | tf_op jit(solution)/shard_map/all_gather | solution.py:12
  216.5 0.9 slice_bitcast_fusion.1
  217.4 22.4 %while.19 = (s32[]{:T(128)}, f32[4,5,2,4]{1,3,2,0:T(4,128)S(1)}, f32[4,5,2,4]{1,3,2,0:T(4,128)S(1)}, f32[4,5,2,4,128]{4,3,2,1,0:T(4,128)S(1)}, f32[16,4,5,2,4]{2...) while((s32[]{:T(128)}, f32[4,5,2,4]{1,3,2,0:T(4,128)S(1)}, ...), condition=%wide.region_15.16_spmd, body=%wide.region_14.15_spmd.sunk | while | flops 62405 | bytes 254871 | solution.py:17
  217.7 1.2 fusion.123
  219.2 1.2 fusion.123
  220.7 1.2 fusion.123
  222.2 1.2 fusion.123
  223.7 1.2 fusion.123
  225.2 1.2 fusion.123
  226.7 1.2 fusion.123
  228.2 1.2 fusion.123
  229.7 1.2 fusion.123
  231.2 1.2 fusion.123
  232.7 1.2 fusion.123
  234.2 1.2 fusion.123
  235.7 1.2 fusion.123
  237.2 1.2 fusion.123
  238.7 1.2 fusion.123
  240.0 0.6 gather_fusion.2
  240.8 0.6 gather_fusion.3
  242.1 0.6 gather_fusion.1
  242.7 2.7 fusion.24
  245.4 38.6 %all_gather.36 = bf16[256,1024]{1,0:T(8,128)(2,1)S(1)} all-gather(bf16[16,1024]{1,0:T(8,128)(2,1)S(1)} %convert_element_type.68), channel_id=1, replica_groups=mesh['groups'=1,'role'=2,'dev'=16] {'dev'}, dimensions={0}, use_global_device_ids=true | all-gather | bytes 557056 | tf_op jit(solution)/shard_map/all_gather | solution.py:203
  284.0 1.0 fusion.114
  285.1 5.3 %reduce-scatter.2.cloned.1.call-done = f32[128,256]{1,0:T(8,128)} async-done(((f32[256,256]{1,0:T(8,128)}), f32[128,256]{1,0:T(8,128)}) %reduce-scatter.2.cloned.1.call-update) | async-done | bytes 131088 | tf_op jit(solution)/shard_map/reduce_scatter | solution.py:207
  290.4 1.5 convert_element_type.69
  (132 shorter events, 10.2 us)
Async XLA Ops:
  7.2 276.9 %copy-start = (bf16[8,128,256]{2,1,0:T(8,128)(2,1)S(1)}, bf16[8,128,256]{2,1,0:T(8,128)(2,1)}, u32[]{:S(2)}) copy-start(bf16[8,128,256]{2,1,0:T(8,128)(2,1)} %param.25) | copy-start | bytes 1572868
  7.2 209.3 %all-gather.2.cloned.1.call-start = ((), (), s32[]{:S(2)}) async-start(), calls=%async_computation.1 | async-start | bytes 1392640 | tf_op jit(solution)/shard_map/all_gather | solution.py:12
  106.7 6.6 %copy-start.1 = (bf16[256,4096]{1,0:T(8,128)(2,1)S(1)}, bf16[256,4096]{1,0:T(8,128)(2,1)}, u32[]{:S(2)}) copy-start(bf16[256,4096]{1,0:T(8,128)(2,1)} %param.15) | copy-start | bytes 6291460
  106.7 7.1 %copy-start.7 = (f32[4096]{0:T(1024)S(1)}, f32[4096]{0:T(1024)}, u32[]{:S(2)}) copy-start(f32[4096]{0:T(1024)} %param.16) | copy-start | bytes 49156
  125.3 0.6 copy-start.2
  125.9 10.3 %copy-start.6 = (s32[16]{0:T(128)S(1)}, s32[16]{0:T(128)}, u32[]{:S(2)}) copy-start(s32[16]{0:T(128)} %param.24) | copy-start | bytes 196
  125.9 10.3 %copy-start.5 = (bf16[16,8,128]{2,1,0:T(8,128)(2,1)S(1)}, bf16[16,8,128]{2,1,0:T(8,128)(2,1)}, u32[]{:S(2)}) copy-start(bf16[16,8,128]{2,1,0:T(8,128)(2,1)} %param.21) | copy-start | bytes 98308
  126.0 13.4 %copy-start.3 = (bf16[16,2,2,128]{3,2,1,0:T(2,128)(2,1)S(1)}, bf16[16,2,2,128]{3,2,1,0:T(2,128)(2,1)}, u32[]{:S(2)}) copy-start(bf16[16,2,2,128]{3,2,1,0:T(2,128)(2,1)} %param.22) | copy-start | bytes 49156
  126.0 164.4 %reduce-scatter.2.cloned.1.call-start = ((), (), s32[]{:S(2)}) async-start(), calls=%async_computation.2 | async-start | bytes 393216 | tf_op jit(solution)/shard_map/reduce_scatter | solution.py:207
  245.4 46.5 %copy-start.4 = (bf16[16,2,4,128]{3,2,1,0:T(4,128)(2,1)}, bf16[16,2,4,128]{3,2,1,0:T(4,128)(2,1)S(1)}, u32[]{:S(2)}) copy-start(bf16[16,2,4,128]{3,2,1,0:T(4,128)(2,1)S(1)} %fusion.24) | copy-start | bytes 98308
Sparse Core Ops, SparseCore 0:
  126.1 53.9 all-gather.1
  285.2 5.1 reduce-scatter.1
where the time goes:
time: 300 us; the launch traced here: 299 us
  blocking collectives  194 us (65%)
  local copies, waits for them, and re-layouts  37.2 us (12%)
  other arithmetic  29.3 us (10%)
  between operations  20.1 us (7%)
  matrix products  12 us (4%)
  waiting for transfers between devices  5.37 us (2%)
    psum x1, blocking collectives, on_device(): table = lax.psum(table, 'dev').astype(jnp.bfloat16)  79.5 us
    all_gather x2, blocking collectives, merged_2(): gathered = jax.tree.map(lambda a: lax.all_gather(a, axis), part)  76.3 us
    all_gather x1, blocking collectives, on_device(): lax.all_gather(flat, 'dev', axis=0, tiled=True)  38.6 us
    add x15, other arithmetic, combine(): first[2] * left_scale[..., None] + second[2] * right_scale[..., None]  17.5 us
    slice x1, local copies, waits for them, and re-layouts, on_device(): response_cache[:, :, :, 0]  10.2 us
    reshape x1, local copies, waits for them, and re-layouts, on_device(): kv_weight.reshape(width, local_heads * 2 * head_size)  7.22 us
    dot_general x1, local copies, waits for them, and re-layouts, on_device(): jnp.dot(normed, kv_weight.reshape(width, local_heads * 2 * head_size), pr...  6.6 us
  transfers between devices with their start and end apart: 2, of which 1 were waited for; matrix products, arithmetic and copies ran while one was open for 5% of the time, Pallas kernels for 0%

commit v1 on v0

--- a/solution.py
+++ b/solution.py
@@ -200,7 +200,9 @@
     flat = attended.reshape(slots, query_heads * head_size)
     weight_flat = out_weight.reshape(query_heads * head_size, out_weight.shape[2])
     head_terms = jnp.dot(
-        lax.all_gather(flat, "dev", axis=0, tiled=True),
+        jnp.concatenate(
+            lax.all_to_all(jnp.stack([flat] * lax.axis_size("dev")), "dev", 0, 0), axis=0
+        ),
         weight_flat,
         preferred_element_type=jnp.float32,
     )

time: 300 us -> 276 us (0.920)
  blocking collectives: 194 us -> 169 us
    all_gather x1 -> x0, blocking collectives: 38.6 us -> none  [on_device(): lax.all_gather(flat, 'dev', axis=0, tiled=True)]
    all_to_all x0 -> x1, blocking collectives: none -> 13.4 us  [on_device(): lax.all_to_all(jnp.stack([flat] * lax.axis_size('dev')), 'dev', 0, 0)]
where the time goes in v1:
time: 276 us; the launch traced here: 275 us
  blocking collectives  169 us (61%)
  local copies, waits for them, and re-layouts  37.4 us (14%)
  other arithmetic  29.3 us (11%)
  between operations  20.1 us (7%)
  matrix products  12 us (4%)
  waiting for transfers between devices  6.32 us (2%)
    psum x1, blocking collectives, on_device(): table = lax.psum(table, 'dev').astype(jnp.bfloat16)  79.5 us
    all_gather x2, blocking collectives, merged_2(): gathered = jax.tree.map(lambda a: lax.all_gather(a, axis), part)  76.2 us
    add x15, other arithmetic, combine(): first[2] * left_scale[..., None] + second[2] * right_scale[..., None]  17.5 us
    all_to_all x1, blocking collectives, on_device(): lax.all_to_all(jnp.stack([flat] * lax.axis_size('dev')), 'dev', 0, 0)  13.4 us
    slice x1, local copies, waits for them, and re-layouts, on_device(): response_cache[:, :, :, 0]  10.3 us
    reshape x1, local copies, waits for them, and re-layouts, on_device(): kv_weight.reshape(width, local_heads * 2 * head_size)  7.22 us
    dot_general x1, local copies, waits for them, and re-layouts, on_device(): jnp.dot(normed, kv_weight.reshape(width, local_heads * 2 * head_size), pr...  6.6 us
    reduce_scatter x1, waiting for transfers between devices, on_device(): lax.psum_scatter(head_terms, 'role', scatter_dimension=0, tiled=True)  6.27 us
  transfers between devices with their start and end apart: 2, of which 1 were waited for; matrix products, arithmetic and copies ran while one was open for 5% of the time, Pallas kernels for 0%

profile of v1, /device:TPU:0, one launch (start us, length us, event | category | flops | bytes accessed | tf_op | source)
XLA Modules:
  0.0 274.7 jit_solution(7736125478416696819)
XLA Ops:
  7.8 0.7 broadcast_add_fusion
  8.6 1.9 bitcast_subtract_fusion.3
  11.8 0.7 broadcast_compare_fusion
  12.5 0.9 select_reduce_fusion.2
  13.4 1.3 fusion.107
  14.8 0.6 fusion.110
  16.3 0.7 fusion.109
  17.0 0.6 fusion.108
  17.6 0.7 add.228
  18.4 0.7 gather_fusion
  19.0 0.9 fusion.46
  19.9 79.5 %psum.7 = bf16[20,1024]{1,0:T(8,128)(2,1)S(1)} all-reduce(f32[20,1024]{1,0:T(8,128)S(1)} %fusion.46), channel_id=1, replica_groups=mesh['groups'=1,'role'=2,'dev'=16] {'dev'}, use_global_device_ids=true, to_apply=%region_9.10 | all-reduce | flops 20480 | bytes 122880 | tf_op jit(solution)/shard_map/psum | solution.py:156
  99.5 7.2 %reshape.416 = bf16[4096,512]{1,0:T(8,128)(2,1)} reshape(bf16[4096,2,2,128]{3,2,1,0:T(2,128)(2,1)} %param.17) | data formatting | bytes 8388608 | tf_op jit(solution)/shard_map/reshape | solution.py:125
  106.7 6.6 %copy.138 = bf16[512,4096]{1,0:T(8,128)(2,1)} copy(bf16[512,4096]{0,1:T(8,128)(2,1)} %bitcast.223) | data formatting | bytes 8388608 | tf_op jit(solution)/shard_map/dot_general | solution.py:123
  113.8 3.6 %fusion.7 = f32[256,2,2,128]{0,3,2,1:T(8,128)S(1)} fusion(bf16[2,2,128,4096]{3,2,1,0:T(8,128)(2,1)} %bitcast.224, bf16[256,4096]{1,0:T(8,128)(2,1)S(1)} %copy-done.1, f32[4096]{0:T(1024)S(1)} %copy-done.7, f32[256]{0:T(256)S(1)} %add_rsqrt_fusion), kind=kOutput, calls=%fused_computation.18 | convolution fusion | flops 1077936128 | bytes 6833152 | tf_op jit(solution)/shard_map/dot_general | solution.py:123
  119.9 1.2 compare_and_fusion
  122.0 0.6 compare_and_fusion.3
  124.1 0.6 compare_and_fusion.1
  125.3 0.6 copy-done.2
  126.0 10.3 %fusion.106 = (bf16[16,256,2,1,128]{4,3,2,1,0:T(2,128)(2,1)}, bf16[16,256,2,1,128]{4,3,2,1,0:T(2,128)(2,1)}) fusion(bf16[16,256,2,2,128]{4,3,2,1,0:T(2,128)(2,1)} %param.23), kind=kLoop, calls=%fused_computation.189 | loop fusion | bytes 8388608 | tf_op jit(solution)/shard_map/slice | solution.py:138
  136.5 2.9 %fusion.111 = (f32[16,2,4]{2,1,0:T(2,128)S(1)}, f32[16,2,4,256]{3,2,1,0:T(4,128)S(1)}) fusion(bf16[16,2,4,128]{3,2,1,0:T(4,128)(2,1)S(1)} %bitcast.234, bf16[16,256,2,1,128]{4,3,2,1,0:T(2,128)(2,1)} %get-tuple-element.211, pred[16,256]{1,0:T(8,128)(4,1)S(1)} %iota_compare_fusion), kind=kOutput, calls=%fused_computation.194 | convolution fusion | flops 8486784 | bytes 2265600 | tf_op jit(solution)/shard_map/sngd,slnd->sngl/dot_general | solution.py:72
  140.3 37.5 %all_gather.29 = f32[16,4,5,2,4]{2,4,3,1,0:T(4,128)S(1)} all-gather(f32[1,4,5,2,4]{2,4,3,1,0:T(4,128)S(1)} %get-tuple-element.219), channel_id=1, replica_groups=mesh['groups'=1,'role'=2,'dev'=16] {'dev'}, dimensions={0}, use_global_device_ids=true | all-gather | bytes 10880 | tf_op jit(solution)/shard_map/all_gather | solution.py:12
  177.8 38.8 %all_gather.26 = f32[16,4,5,2,4]{2,4,3,1,0:T(4,128)S(1)} all-gather(f32[1,4,5,2,4]{2,4,3,1,0:T(4,128)S(1)} %get-tuple-element.220), channel_id=1, replica_groups=mesh['groups'=1,'role'=2,'dev'=16] {'dev'}, dimensions={0}, use_global_device_ids=true | all-gather | bytes 10880 | tf_op jit(solution)/shard_map/all_gather | solution.py:12
  216.6 0.9 slice_bitcast_fusion.1
  217.5 22.4 %while.19 = (s32[]{:T(128)}, f32[4,5,2,4]{1,3,2,0:T(4,128)S(1)}, f32[4,5,2,4]{1,3,2,0:T(4,128)S(1)}, f32[4,5,2,4,128]{4,3,2,1,0:T(4,128)S(1)}, f32[16,4,5,2,4]{2...) while((s32[]{:T(128)}, f32[4,5,2,4]{1,3,2,0:T(4,128)S(1)}, ...), condition=%wide.region_15.16_spmd, body=%wide.region_14.15_spmd.sunk | while | flops 62405 | bytes 254871 | solution.py:17
  217.8 1.2 fusion.123
  219.3 1.2 fusion.123
  220.8 1.2 fusion.123
  222.3 1.2 fusion.123
  223.8 1.2 fusion.123
  225.3 1.2 fusion.123
  226.8 1.2 fusion.123
  228.3 1.2 fusion.123
  229.8 1.2 fusion.123
  231.3 1.2 fusion.123
  232.8 1.2 fusion.123
  234.3 1.2 fusion.123
  235.8 1.2 fusion.123
  237.3 1.2 fusion.123
  238.8 1.2 fusion.123
  240.1 0.6 gather_fusion.2
  240.9 0.6 gather_fusion.3
  242.2 0.6 gather_fusion.1
  242.8 2.7 fusion.24
  245.6 13.4 %all_to_all.5 = bf16[16,16,1024]{2,1,0:T(8,128)(2,1)S(1)} all-to-all(bf16[16,16,1024]{2,1,0:T(8,128)(2,1)S(1)} %stack.3), channel_id=1, replica_groups=mesh['groups'=1,'role'=2,'dev'=16] {'dev'}, dimensions={0} | all-to-all | bytes 1048576 | tf_op jit(solution)/shard_map/all_to_all | solution.py:204
  259.0 1.0 fusion.114
  260.0 6.3 %reduce-scatter.2.cloned.1.call-done = f32[128,256]{1,0:T(8,128)} async-done(((f32[256,256]{1,0:T(8,128)}), f32[128,256]{1,0:T(8,128)}) %reduce-scatter.2.cloned.1.call-update) | async-done | bytes 131088 | tf_op jit(solution)/shard_map/reduce_scatter | solution.py:209
  266.3 1.5 convert_element_type.70
  (133 shorter events, 10.2 us)
Async XLA Ops:
  7.2 251.8 %copy-start = (bf16[8,128,256]{2,1,0:T(8,128)(2,1)S(1)}, bf16[8,128,256]{2,1,0:T(8,128)(2,1)}, u32[]{:S(2)}) copy-start(bf16[8,128,256]{2,1,0:T(8,128)(2,1)} %param.25) | copy-start | bytes 1572868
  7.2 209.5 %all-gather.2.cloned.1.call-start = ((), (), s32[]{:S(2)}) async-start(), calls=%async_computation.2 | async-start | bytes 1392640 | tf_op jit(solution)/shard_map/all_gather | solution.py:12
  106.7 6.6 %copy-start.1 = (bf16[256,4096]{1,0:T(8,128)(2,1)S(1)}, bf16[256,4096]{1,0:T(8,128)(2,1)}, u32[]{:S(2)}) copy-start(bf16[256,4096]{1,0:T(8,128)(2,1)} %param.15) | copy-start | bytes 6291460
  106.7 7.1 %copy-start.7 = (f32[4096]{0:T(1024)S(1)}, f32[4096]{0:T(1024)}, u32[]{:S(2)}) copy-start(f32[4096]{0:T(1024)} %param.16) | copy-start | bytes 49156
  125.3 0.6 copy-start.2
  125.9 10.4 %copy-start.6 = (s32[16]{0:T(128)S(1)}, s32[16]{0:T(128)}, u32[]{:S(2)}) copy-start(s32[16]{0:T(128)} %param.24) | copy-start | bytes 196
  125.9 10.5 %copy-start.5 = (bf16[16,8,128]{2,1,0:T(8,128)(2,1)S(1)}, bf16[16,8,128]{2,1,0:T(8,128)(2,1)}, u32[]{:S(2)}) copy-start(bf16[16,8,128]{2,1,0:T(8,128)(2,1)} %param.21) | copy-start | bytes 98308
  126.0 13.5 %copy-start.3 = (bf16[16,2,2,128]{3,2,1,0:T(2,128)(2,1)S(1)}, bf16[16,2,2,128]{3,2,1,0:T(2,128)(2,1)}, u32[]{:S(2)}) copy-start(bf16[16,2,2,128]{3,2,1,0:T(2,128)(2,1)} %param.22) | copy-start | bytes 49156
  126.0 140.3 %reduce-scatter.2.cloned.1.call-start = ((), (), s32[]{:S(2)}) async-start(), calls=%async_computation.3 | async-start | bytes 393216 | tf_op jit(solution)/shard_map/reduce_scatter | solution.py:209
  245.5 22.3 %copy-start.4 = (bf16[16,2,4,128]{3,2,1,0:T(4,128)(2,1)}, bf16[16,2,4,128]{3,2,1,0:T(4,128)(2,1)S(1)}, u32[]{:S(2)}) copy-start(bf16[16,2,4,128]{3,2,1,0:T(4,128)(2,1)S(1)} %fusion.24) | copy-start | bytes 98308
Sparse Core Ops, SparseCore 0:
  126.1 53.9 all-gather.1
  260.2 6.1 reduce-scatter.1
